TPU v7x, 768 devices: a whole 4x8x12 slice. The times are simulated.
768 devices in a mesh: group: 12 (over z), tensor: 4 (over y_lo), role: 16 (over y_hi, x, core).
Axes of the slice: x: 4, y: 8 (y_hi: 2, y_lo: 4; y = y_hi * 4 + y_lo), z: 12, core: 2. Of those that a mesh axis runs over, the one named last changes fastest.
Arguments:
- tokens: bfloat16 [12, 4096, 2880], P('group', 'role'), may hold values from -6 to 6
- gain: float32 [2880], replicated, may hold values from 0.1 to 1.9
- q_weight: bfloat16 [2880, 2048], P(('group', 'role'), 'tensor'), may hold values from -0.109375 to 0.109375
- kv_weight: bfloat16 [2880, 512], P(('group', 'role'), 'tensor'), may hold values from -0.109375 to 0.109375
- out_weight: bfloat16 [2048, 2880], P('role', 'tensor'), may hold values from -0.5 to 0.5
- sinks: float32 [32], P('tensor'), may hold values from -1 to 3
- segments: int32 [12, 4096], P('group', 'role'), may hold values from 0 to 31, never falling along the last dimension, each value on 1 to 2304 neighbouring positions
Outputs:
- mixed: bfloat16 [12, 4096, 2880], P('group', 'role', 'tensor')
Inputs may be any that keep to these rules, and one draw needn't show every extreme that they name: `segments`: within a group, document numbers never fall along the positions; each document holds 1 to 2304 positions and one holds exactly 2304.
All inputs are finite; a program needn't handle non-finite values.
Results may differ from a plain program's by a relative error of at most 0.009.
Values may be sent and summed in bfloat16 or wider, within the bound.
A program may use at most 64 MiB of HBM per device.

v0:
```python
import jax
import jax.numpy as jnp
from jax import lax
from jax.sharding import PartitionSpec as P

HEAD_DIM = 64


def side_by_side(arrays, axis, dim, along):
    ends, at = ([], 0)
    for a in arrays[:-1]:
        at += a.shape[along]
        ends.append(at)
    both = jnp.concatenate(arrays, axis=along)
    return tuple(jnp.split(lax.all_gather(both, axis, axis=dim, tiled=True), ends, axis=along))


def copy_for_each(array, axis):
    length = lax.axis_size(axis)
    return lax.all_to_all(
        jnp.broadcast_to(array[None], (length, *array.shape)), axis, 0, 0, tiled=True
    )


def laid_out(blocks, dim):
    blocks = jnp.moveaxis(blocks, 0, dim)
    lengths = blocks.shape
    return blocks.reshape(*lengths[:dim], lengths[dim] * lengths[dim + 1], *lengths[dim + 2 :])


def gather_directly(array, axis, dim):
    blocks = copy_for_each(array, axis)
    return laid_out(blocks, dim)


def rotate(vectors, positions):
    half_dim = HEAD_DIM // 2
    frequency = jnp.exp(-jnp.log(150000.0) * jnp.arange(half_dim, dtype=jnp.float32) / half_dim)
    angle = positions[:, None] * frequency[None, :]
    cosine = jnp.cos(angle)[:, None, :]
    sine = jnp.sin(angle)[:, None, :]
    first_half = vectors[..., :half_dim]
    second_half = vectors[..., half_dim:]
    return jnp.concatenate(
        [first_half * cosine - second_half * sine, second_half * cosine + first_half * sine],
        axis=-1,
    )


def on_device(tokens, gain, q_weight, kv_weight, out_weight, sinks, segments):
    feature = tokens[0]
    doc_ids = segments[0]
    rows_here = feature.shape[0]
    widened = feature.astype(jnp.float32)
    normed = (
        widened * lax.rsqrt(jnp.mean(widened * widened, axis=-1, keepdims=True) + 1e-05) * gain
    ).astype(jnp.bfloat16)
    query_width = q_weight.shape[1]
    pair_width = kv_weight.shape[1]

    def add_rows(piece):
        return jnp.dot(normed, piece, preferred_element_type=jnp.float32)

    pieces = side_by_side((q_weight, kv_weight), ("group", "role"), 0, 1)
    query_sum = add_rows(pieces[0])
    pair_sum = add_rows(pieces[1])
    local_heads = query_width // HEAD_DIM
    local_pairs = pair_width // (2 * HEAD_DIM)
    group_size = local_heads // local_pairs
    first_pos = lax.axis_index("role") * rows_here
    own_pos = first_pos + jnp.arange(rows_here, dtype=jnp.int32)
    positions = own_pos.astype(jnp.float32)
    queries = rotate(query_sum.reshape(rows_here, local_heads, HEAD_DIM), positions).astype(
        jnp.bfloat16
    )
    queries = queries.reshape(rows_here, local_pairs, group_size, HEAD_DIM)
    paired = pair_sum.reshape(rows_here, local_pairs, 2, HEAD_DIM)
    key_rows = rotate(paired[:, :, 0], positions).astype(jnp.bfloat16)
    value_rows = paired[:, :, 1].astype(jnp.bfloat16)
    packed = jnp.stack([key_rows, value_rows], axis=2).reshape(rows_here, pair_width)
    last_pos = first_pos + rows_here - 1
    first_doc = doc_ids[0]

    def attend_block(running, packed_block, doc_block, first_key):
        key_count = doc_block.shape[0]
        key_block = packed_block.reshape(key_count, local_pairs, 2, HEAD_DIM)

        def compute(current):
            scores = (
                jnp.einsum(
                    "tkgd,nkd->kgtn",
                    queries,
                    key_block[:, :, 0],
                    preferred_element_type=jnp.float32,
                )
                * 0.125
            )
            key_pos = first_key + jnp.arange(key_count, dtype=jnp.int32)
            allowed = (key_pos[None, :] <= own_pos[:, None]) & (
                doc_block[None, :] == doc_ids[:, None]
            )
            weights = jnp.where(allowed[None, None], jnp.exp(scores), 0.0)
            added = jnp.einsum(
                "kgtn,nkd->tkgd",
                weights.astype(jnp.bfloat16),
                key_block[:, :, 1],
                preferred_element_type=jnp.float32,
            )
            return (current[0] + jnp.sum(weights, axis=-1), current[1] + added)

        useless = (first_key > last_pos) | (doc_block[-1] < first_doc)
        return lax.cond(useless, lambda current: current, compute, running)

    initial = (
        jnp.zeros((local_pairs, group_size, rows_here), jnp.float32),
        jnp.zeros((rows_here, local_pairs, group_size, HEAD_DIM), jnp.float32),
    )
    running = initial
    packed_piece = gather_directly(packed, "role", 0)
    doc_piece = gather_directly(doc_ids, "role", 0)
    key_count = doc_piece.shape[0]
    blocks = key_count // 512

    def advance(current, element):
        block_packed, block_docs, offset = element
        return (attend_block(current, block_packed, block_docs, offset * 512), None)

    running, unused = lax.scan(
        advance,
        running,
        (
            packed_piece.reshape(blocks, 512, pair_width),
            doc_piece.reshape(blocks, 512),
            jnp.arange(blocks, dtype=jnp.int32),
        ),
    )
    denoms, numerators = running
    denoms = denoms + jnp.exp(sinks).reshape(local_pairs, group_size)[:, :, None]
    context = (
        (numerators / jnp.transpose(denoms, (2, 0, 1))[..., None])
        .astype(jnp.bfloat16)
        .reshape(rows_here, query_width)
    )
    all_heads = gather_directly(context, "tensor", 1)
    mixed = jnp.dot(
        all_heads,
        lax.all_gather(out_weight, "role", axis=0, tiled=True),
        preferred_element_type=jnp.float32,
    )
    return mixed.astype(jnp.bfloat16)[None]


def solution(mesh):
    placed = (
        P("group", "role", None),
        P(),
        P(("group", "role"), "tensor"),
        P(("group", "role"), "tensor"),
        P("role", "tensor"),
        P("tensor"),
        P("group", "role"),
    )
    return jax.shard_map(
        on_device,
        mesh=mesh,
        in_specs=placed,
        out_specs=P("group", "role", "tensor"),
        check_vma=False,
    )
```

profile of v0, /device:TPU:60, one launch (start us, length us, event | category | flops | bytes accessed | tf_op | source)
XLA Modules:
  0.0 323.8 jit_solution(208862759876306499)
XLA Ops:
  6.5 1.3 maximum_bitcast_fusion
  7.9 1.3 broadcast_in_dim.36
  9.2 9.6 %all-to-all-start = ((s32[16,1,256]{2,1,0:T(1,128)}), s32[16,1,256]{2,1,0:T(1,128)S(1)}, u32[]{:S(2)}, u32[]{:S(2)}) async-start(s32[16,1,256]{2,1,0:T(1,128)} %broadcast_in_dim.36), calls=%async_computation | async-start | bytes 32768 | tf_op jit(solution)/shard_map/all_to_all | solution.py:20
  19.6 1.8 fusion.20
  21.4 178.8 %all-gather.6.cloned.1.call-done = bf16[192,15,640]{2,1,0:T(8,128)(2,1)} async-done(((bf16[1,15,640]{2,1,0:T(8,128)(2,1)}), bf16[192,15,640]{2,1,0:T(8,128)(2,1)}) %all-gather.6.cloned.1.call-update) | async-done | bytes 3686416 | tf_op jit(solution)/shard_map/all_gather | solution.py:15
  200.2 6.0 %reshape.353 = bf16[2880,640]{1,0:T(8,128)(2,1)} reshape(bf16[192,15,640]{2,1,0:T(8,128)(2,1)} %all-gather.6.cloned.1.call-done) | data formatting | bytes 7372800
  206.2 1.3 slice_bitcast_fusion.5
  208.9 1.3 broadcast_in_dim.38
  210.2 9.6 %all-to-all-start.1 = ((bf16[16,256,128]{2,1,0:T(8,128)(2,1)}), bf16[16,256,128]{2,1,0:T(8,128)(2,1)}, u32[]{:S(2)}, u32[]{:S(2)}) async-start(bf16[16,256,128]{2,1,0:T(8,128)(2,1)} %broadcast_in_dim.38), calls=%async_computation.1 | async-start | bytes 2097152 | tf_op jit(solution)/shard_map/all_to_all | solution.py:20
  220.7 2.0 slice_bitcast_fusion.4
  222.7 3.0 copy.21
  225.7 3.4 %fusion.25 = f32[256,8,64]{0,2,1:T(8,128)S(1)} fusion(bf16[8,64,2880]{2,1,0:T(8,128)(2,1)} %bitcast.101, bf16[1,256,2880]{1,2,0:T(8,128)(2,1)} %param.11, f32[2880]{0:T(1024)S(1)} %copy-done.2, f32[256]{0:T(256)S(1)} %add_rsqrt_fusion), kind=kOutput, calls=%fused_computation.35 | convolution fusion | flops 757923840 | bytes 4960512 | tf_op jit(solution)/shard_map/dot_general | solution.py:62
  229.3 6.2 %all-to-all-done.1 = bf16[16,256,128]{2,1,0:T(8,128)(2,1)} async-done(((bf16[16,256,128]{2,1,0:T(8,128)(2,1)}), bf16[16,256,128]{2,1,0:T(8,128)(2,1)}, u32[]{:S(2)}, u32[]{:S(2)}) %all-to-all-start.1) | async-done | bytes 1048608 | tf_op jit(solution)/shard_map/all_to_all | solution.py:20
  235.4 1.5 copy.22
  237.0 33.6 %while.13 = (s32[]{:T(128)}, f32[1,8,256]{2,1,0:T(8,128)S(1)}, f32[256,1,8,64]{0,3,2,1:T(8,128)S(1)}, s32[8]{0:T(128)S(1)}, s32[]{:T(128)}, /*index=5*/s32[8,512...) while((s32[]{:T(128)}, f32[1,8,256]{2,1,0:T(8,128)S(1)}, ...), condition=%wide.region_5.6_spmd.clone, body=%wide.region_1.5_spmd.clone.sunk | while | flops 275251968 | bytes 10534239 | solution.py:128
  249.2 2.3 conditional.3
  249.5 1.1 fusion.3
  254.6 2.3 conditional.3
  259.9 2.3 conditional.3
  260.2 1.1 fusion.3
  265.2 2.3 conditional.3
  271.8 17.6 %all-to-all-start.2 = ((bf16[4,256,512]{1,2,0:T(8,128)(2,1)}), bf16[4,256,512]{1,2,0:T(8,128)(2,1)S(1)}, u32[]{:S(2)}, u32[]{:S(2)}) async-start(bf16[4,256,512]{1,2,0:T(8,128)(2,1)} %broadcast_in_dim.63), calls=%async_computation.2 | async-start | bytes 2097152 | tf_op jit(solution)/shard_map/all_to_all | solution.py:20
  289.3 24.2 %all-to-all-done.2 = bf16[4,256,512]{1,2,0:T(8,128)(2,1)S(1)} async-done(((bf16[4,256,512]{1,2,0:T(8,128)(2,1)}), bf16[4,256,512]{1,2,0:T(8,128)(2,1)S(1)}, u32[]{:S(2)}, u32[]{:S(2)}) %all-to-all-start.2) | async-done | bytes 1048608 | tf_op jit(solution)/shard_map/all_to_all | solution.py:20
  313.5 3.5 %fusion.24 = bf16[1,256,720]{1,2,0:T(8,128)(2,1)} fusion(bf16[2048,720]{0,1:T(8,128)(2,1)} %all-gather.4.cloned.1.call-done, bf16[256,2048]{0,1:T(8,128)(2,1)S(1)} %bitcast.103), kind=kOutput, calls=%fused_computation.31 | convolution fusion | flops 755159040 | bytes 4366336 | tf_op jit(solution)/shard_map/dot_general | solution.py:145
  (99 shorter events, 20.6 us)
Async XLA Ops:
  6.5 193.6 %all-gather.6.cloned.1.call-start = ((), (), s32[]{:S(2)}) async-start(), calls=%async_computation.4 | async-start | bytes 3952640 | tf_op jit(solution)/shard_map/all_gather | solution.py:15
  9.2 199.7 %all-to-all-start = ((s32[16,1,256]{2,1,0:T(1,128)}), s32[16,1,256]{2,1,0:T(1,128)S(1)}, u32[]{:S(2)}, u32[]{:S(2)}) async-start(s32[16,1,256]{2,1,0:T(1,128)} %broadcast_in_dim.36), calls=%async_computation | async-start | bytes 32768 | tf_op jit(solution)/shard_map/all_to_all | solution.py:20
  18.8 270.5 %all-gather.4.cloned.1.call-start = ((), (), s32[]{:S(2)}) async-start(), calls=%async_computation.3 | async-start | bytes 3133440 | tf_op jit(solution)/shard_map/all_gather | solution.py:147
  206.2 1.6 copy-start
  206.2 1.6 copy-start.2
  207.8 12.0 %copy-start.1 = (s32[1,256]{1,0:T(1,128)S(1)}, s32[1,256]{1,0:T(1,128)}, u32[]{:S(2)}) copy-start(s32[1,256]{1,0:T(1,128)} %param.17) | copy-start | bytes 3076
  207.9 12.6 %copy-start.3 = (f32[8]{0:T(128)S(1)}, f32[8]{0:T(128)}, u32[]{:S(2)}) copy-start(f32[8]{0:T(128)} %param.16) | copy-start | bytes 100
  210.2 25.3 %all-to-all-start.1 = ((bf16[16,256,128]{2,1,0:T(8,128)(2,1)}), bf16[16,256,128]{2,1,0:T(8,128)(2,1)}, u32[]{:S(2)}, u32[]{:S(2)}) async-start(bf16[16,256,128]{2,1,0:T(8,128)(2,1)} %broadcast_in_dim.38), calls=%async_computation.1 | async-start | bytes 2097152 | tf_op jit(solution)/shard_map/all_to_all | solution.py:20
  271.8 41.7 %all-to-all-start.2 = ((bf16[4,256,512]{1,2,0:T(8,128)(2,1)}), bf16[4,256,512]{1,2,0:T(8,128)(2,1)S(1)}, u32[]{:S(2)}, u32[]{:S(2)}) async-start(bf16[4,256,512]{1,2,0:T(8,128)(2,1)} %broadcast_in_dim.63), calls=%async_computation.2 | async-start | bytes 2097152 | tf_op jit(solution)/shard_map/all_to_all | solution.py:20
Sparse Core Ops, SparseCore 0:
  12.9 187.1 all-gather.5
  203.9 80.0 all-gather.3
where the time goes:
time: 328 us; the launch traced here: 324 us
  waiting for transfers between devices  210 us (64%)
  starting transfers between devices  36.9 us (11%)
  local copies, waits for them, and re-layouts  28.2 us (9%)
  matrix products  15.5 us (5%)
  loops' own time  15.2 us (5%)
  between operations  13.6 us (4%)
  other arithmetic  4.7 us (1%)
    all_gather x1, waiting for transfers between devices, side_by_side(): lax.all_gather(both, axis, axis=dim, tiled=True)  179 us
    all_to_all x3, starting transfers between devices, copy_for_each(): lax.all_to_all(jnp.broadcast_to(array[None], (length, *array.shape)), axi...  36.8 us
    all_to_all x3, waiting for transfers between devices, copy_for_each(): lax.all_to_all(jnp.broadcast_to(array[None], (length, *array.shape)), axi...  30.3 us
    another operation x1, loops' own time, on_device(): lax.scan(advance, running, (packed_piece.reshape(blocks, 512, pair_width)...  14.9 us
    unnamed x10, local copies, waits for them, and re-layouts  7.52 us
    dot_general x4, local copies, waits for them, and re-layouts, add_rows(): return jnp.dot(normed, piece, preferred_element_type=jnp.float32)  6.69 us
  transfers between devices with their start and end apart: 5, of which 3 were waited for; matrix products, arithmetic and copies ran while one was open for 13% of the time, Pallas kernels for 0%

commit v1 on v0

v1 whole, which is shorter than its diff:
```python
import functools
import math

import jax
import jax.numpy as jnp
import numpy as np
from jax import lax
from jax.experimental import pallas as pl
from jax.experimental.pallas import tpu as pltpu
from jax.sharding import PartitionSpec as P

HEAD_DIM = 64
REACH = 9
CHUNKS = 4
NEG = -1e30
LOG2E = 1.4426950408889634
F32 = jnp.float32
BF16 = jnp.bfloat16


def kernel(
    dims,
    tokens,
    gain,
    w_in,
    wo_in,
    seg_rows,
    seg_cols,
    sink_exp,
    near_cos,
    near_sin,
    far_cos,
    far_sin,
    out,
    normed,
    spread,
    w_all,
    acc,
    q_all,
    kv_all,
    bias,
    o_acc,
    wo_all,
    ctx,
    out_acc,
    plane_send,
    plane_recv,
    ring_send,
    ring_recv,
    twin_send,
    twin_recv,
    ctx_send,
    ctx_recv,
):
    NG, NT, R, NX, ROWS, D = dims
    HALF = R // 2
    H = NG // 2
    PAIRS = q_all.shape[0] // 2
    WIDE = q_all.shape[0] * HEAD_DIM
    PER = HALF // CHUNKS
    g = lax.axis_index("group")
    t = lax.axis_index("tensor")
    r = lax.axis_index("role")
    c = lax.rem(r, 2)
    x = lax.rem(r // 2, NX)
    yh = r // HALF

    def role_of(y_, x_, c_):
        return y_ * HALF + x_ * 2 + c_

    def x_at(dx):
        return lax.rem(x + dx, NX)

    twin = {"role": role_of(yh, x, 1 - c)}
    across = {"role": role_of(1 - yh, x, c)}

    def x_to(dx):
        return {"role": role_of(yh, x_at(dx), c)}

    up = lax.rem(g + 1, NG)
    down = lax.rem(g + NG - 1, NG)

    def remote(src, dst, send, recv, where):
        return pltpu.make_async_remote_copy(
            src_ref=src,
            dst_ref=dst,
            send_sem=send,
            recv_sem=recv,
            device_id=where,
            device_id_type=pl.DeviceIdType.MESH,
        )

    greeted = [twin, across, {"group": up}, {"group": down}]
    greeted += [x_to(dx) for dx in range(1, NX)]
    greeted += [{"tensor": lax.rem(t + dt, NT)} for dt in range(1, NT)]
    barrier = pltpu.get_barrier_semaphore()
    for where in greeted:
        pl.semaphore_signal(
            barrier, inc=1, device_id=where, device_id_type=pl.DeviceIdType.MESH
        )
    pl.semaphore_wait(barrier, len(greeted))

    class Gather:
        def __init__(self, which, own, slot):
            self.send = plane_send.at[which]
            self.recv = plane_recv.at[which]
            self.own = own
            self.slot = slot

        def copy(self, index, role, where, src=None):
            dst = self.slot(role)
            return remote(
                dst if src is None else src, dst, self.send.at[index], self.recv.at[index], where
            )

        def across(self):
            return self.copy(0, r, across, self.own)

        def along(self, dx):
            return self.copy(dx, r, x_to(dx), self.own)

        def along_other(self, dx):
            return self.copy(NX - 1 + dx, role_of(1 - yh, x, c), x_to(dx))

        def twin_near(self, dx):
            if dx == 0:
                return self.copy(2 * NX, r, twin, self.own)
            return self.copy(2 * NX + dx, role_of(yh, lax.rem(x + NX - dx, NX), c), twin)

        def twin_other(self, dx):
            return self.copy(3 * NX + dx, role_of(1 - yh, lax.rem(x + NX - dx, NX), c), twin)

    gather_w = Gather(
        0,
        w_in,
        lambda role: w_all.at[
            g, lax.rem(role, 2) * HALF + (role // HALF) * NX + lax.rem(role // 2, NX)
        ],
    )
    gather_o = Gather(1, wo_in, lambda role: wo_all.at[role])
    gather_k = Gather(2, kv_all.at[r], lambda role: kv_all.at[role])
    offsets = range(1, NX)

    gather_w.across().start()
    for dx in offsets:
        gather_w.along(dx).start()
    gather_w.twin_near(0).start()
    own_slot = c * HALF + yh * NX + x
    w_all[g, own_slot] = w_in[...]
    wo_all[r] = wo_in[...]

    top = (D // 128) * 128
    if normed.shape[1] > top:
        normed[:, top:] = jnp.zeros((ROWS, normed.shape[1] - top), BF16)

    def norm_rows(i, _):
        rows = pl.ds(pl.multiple_of(i * 16, 16), 16)
        wide = tokens[rows, :].astype(F32)
        scale = lax.rsqrt(jnp.sum(wide * wide, axis=-1, keepdims=True) * (1.0 / D) + 1e-05)
        normed[rows, 0:D] = (wide * scale * gain[...]).astype(BF16)
        return 0

    lax.fori_loop(0, ROWS // 16, norm_rows, 0)

    for dx in offsets:
        gather_w.along(dx).wait_recv()
        gather_w.twin_near(dx).start()

    window = spread_window(R)
    lane = lax.broadcasted_iota(jnp.int32, (1, R * 16), 1)
    slot_of = lane // 16
    within = lax.rem(lane, 16)
    slot_role = (
        (lax.rem(slot_of, HALF) // NX) * HALF + lax.rem(slot_of, NX) * 2 + slot_of // HALF
    )
    feature = jnp.where(within < 15, slot_role * 15 + within, -4096)
    row_id = lax.broadcasted_iota(jnp.int32, (window, R * 16), 0)

    def spread_plane(p, _):
        first = p * (15 * R)
        start = (first // 128) * 128
        hit = row_id == (feature + (first - start))
        pick = jnp.where(hit, 1.0, 0.0).astype(BF16)
        part = normed[:, pl.ds(pl.multiple_of(start, 128), window)]
        spread[p] = jnp.dot(part, pick, preferred_element_type=F32).astype(BF16)
        return 0

    lax.fori_loop(0, NG, spread_plane, 0)

    gather_w.across().wait_recv()
    for dx in offsets:
        gather_w.along_other(dx).start()
    gather_w.twin_other(0).start()
    for dx in offsets:
        gather_w.along_other(dx).wait_recv()

    def plane(d, s):
        return lax.rem(g - s + NG, NG) if d == 0 else lax.rem(g + s, NG)

    def ring(d, s, j):
        ref = w_all.at[plane(d, s), pl.ds(c * HALF + j * PER, PER)]
        return remote(
            ref,
            ref,
            ring_send.at[d, s, j],
            ring_recv.at[d, s, j],
            {"group": up if d == 0 else down},
        )

    def twin_plane(d, s):
        ref = w_all.at[plane(d, s), pl.ds(c * HALF, HALF)]
        return remote(ref, ref, twin_send.at[d, s], twin_recv.at[d, s], twin)

    def twin_half(d):
        ref = w_all.at[plane(d, H), pl.ds(c * HALF + d * (HALF // 2), HALF // 2)]
        return remote(ref, ref, twin_send.at[d, H], twin_recv.at[d, H], twin)

    def last_chunks(d):
        return range(d * (CHUNKS // 2), (d + 1) * (CHUNKS // 2))

    def add_plane(p):
        acc[...] += jnp.dot(
            spread[p],
            w_all[p].reshape(R * 16, acc.shape[1]),
            preferred_element_type=F32,
        )

    for j in range(CHUNKS):
        for d in range(2):
            ring(d, 0, j).start()
    for dx in offsets:
        gather_w.twin_other(dx).start()
    gather_o.across().start()
    for dx in offsets:
        gather_o.along(dx).start()
    gather_o.twin_near(0).start()

    for dx in range(NX):
        gather_w.twin_near(dx).wait_recv()
        gather_w.twin_other(dx).wait_recv()
    acc[...] = jnp.zeros_like(acc)
    add_plane(g)

    def turn(s, _):
        for j in range(CHUNKS):
            for d in range(2):
                ring(d, s - 1, j).wait_recv()
                ring(d, s, j).start()
        for d in range(2):
            twin_plane(d, s).start()

        @pl.when(s >= 2)
        def _():
            for d in range(2):
                twin_plane(d, s - 1).wait_recv()
                add_plane(plane(d, s - 1))

        return 0

    if H > 2:
        lax.fori_loop(1, H - 1, turn, 0)
    for j in range(CHUNKS):
        for d in range(2):
            ring(d, H - 2, j).wait_recv()
            if j in last_chunks(d):
                ring(d, H - 1, j).start()
    for d in range(2):
        twin_plane(d, H - 1).start()
    if H > 2:
        for d in range(2):
            twin_plane(d, H - 2).wait_recv()
            add_plane(plane(d, H - 2))
    for d in range(2):
        twin_plane(d, H - 1).wait_recv()
        add_plane(plane(d, H - 1))
    for d in range(2):
        for j in last_chunks(d):
            ring(d, H - 1, j).wait_recv()
        twin_half(d).start()
    for d in range(2):
        twin_half(d).wait_recv()
    add_plane(plane(0, H))

    cos_far = far_cos[pl.ds(r, 1), :]
    sin_far = far_sin[pl.ds(r, 1), :]
    cos = near_cos[...] * cos_far - near_sin[...] * sin_far
    sin = near_sin[...] * cos_far + near_cos[...] * sin_far
    lanes = lax.broadcasted_iota(jnp.int32, (ROWS, 128), 1)
    first_half = lax.rem(lanes, HEAD_DIM) < HEAD_DIM // 2
    low = lanes < HEAD_DIM
    signed = jnp.where(first_half, -sin, sin)

    def swapped(u):
        return jnp.where(
            first_half, pltpu.roll(u, 128 - HEAD_DIM // 2, 1), pltpu.roll(u, HEAD_DIM // 2, 1)
        )

    pair = acc[:, WIDE : WIDE + 128]
    turned = pair * jnp.where(low, cos, 1.0) + swapped(pair) * jnp.where(low, signed, 0.0)
    kv_all[r, 0:ROWS] = turned.astype(BF16)
    kv_all[r, ROWS : ROWS + 16] = seg_rows[...]

    @pl.when(yh == 0)
    def _():
        gather_k.across().start()

    for dx in offsets:
        gather_k.along(dx).start()
    gather_k.twin_near(0).start()

    fold = 0.125 * LOG2E
    for i in range(PAIRS):
        u = acc[:, 128 * i : 128 * (i + 1)]
        turned = (u * cos + swapped(u) * signed) * fold
        q_all[2 * i] = jnp.where(low, turned, 0.0).astype(BF16)
        q_all[2 * i + 1] = jnp.where(low, pltpu.roll(turned, HEAD_DIM, 1), 0.0).astype(BF16)

    q_pos = lax.broadcasted_iota(jnp.int32, (ROWS, 128), 0) + r * ROWS
    k_off = lax.broadcasted_iota(jnp.int32, (ROWS, 128), 1)

    def make_bias(b):
        docs = seg_cols[...].astype(F32)
        for part in range(ROWS // 128):
            keys = kv_all[b, ROWS + part : ROWS + part + 1, :].astype(F32)
            seen = (docs == keys) & (k_off + (b * ROWS + part * 128) <= q_pos)
            bias[b, :, part * 128 : (part + 1) * 128] = jnp.where(seen, 0.0, NEG)

    def attend(b, h, fresh=False):
        block = kv_all[b, 0:ROWS, :]
        scores = lax.dot_general(
            q_all[h], block, (((1,), (1,)), ((), ())), preferred_element_type=F32
        )
        weights = jnp.exp2(scores + bias[b]).astype(BF16)
        lanes_b = lax.broadcasted_iota(jnp.int32, block.shape, 1)
        with_ones = jnp.where(lanes_b < HEAD_DIM, jnp.ones_like(block), block)
        added = jnp.dot(weights, with_ones, preferred_element_type=F32)
        if fresh:
            o_acc[h] = added
        else:
            o_acc[h] += added

    make_bias(r)

    def own_pair(i, _):
        attend(r, 2 * i, True)
        attend(r, 2 * i + 1, True)
        return 0

    lax.fori_loop(0, PAIRS, own_pair, 0)

    for dx in offsets:
        gather_k.along(dx).wait_recv()
        gather_k.twin_near(dx).start()

    @pl.when(yh == 1)
    def _():
        gather_k.across().wait_recv()
        for dx in offsets:
            gather_k.along_other(dx).start()
        gather_k.twin_other(0).start()

    for dx in range(NX):
        gather_k.twin_near(dx).wait_recv()

    def near_block(b, _):
        make_bias(b)

        def of_pair(i, _):
            attend(b, 2 * i)
            attend(b, 2 * i + 1)
            return 0

        lax.fori_loop(0, PAIRS, of_pair, 0)
        return 0

    lax.fori_loop(yh * HALF, r, near_block, 0)

    @pl.when(yh == 1)
    def _():
        for dx in offsets:
            gather_k.along_other(dx).wait_recv()
            gather_k.twin_other(dx).start()

    for dx in offsets:
        gather_o.along(dx).wait_recv()
        gather_o.twin_near(dx).start()
    gather_o.across().wait_recv()
    for dx in offsets:
        gather_o.along_other(dx).start()
    gather_o.twin_other(0).start()

    far_from = jnp.maximum(r - REACH, 0)
    far_to = jnp.where(yh == 1, HALF, far_from)

    @pl.when(yh == 1)
    def _():
        for dx in range(NX):
            gather_k.twin_other(dx).wait_recv()

        def far_bias(b, _):
            make_bias(b)
            return 0

        lax.fori_loop(far_from, HALF, far_bias, 0)

    def ctx_copy(i, dt):
        ref = ctx.at[t, i]
        return remote(
            ref, ref, ctx_send.at[i, dt], ctx_recv.at[i, dt], {"tensor": lax.rem(t + dt, NT)}
        )

    def finish_pair(i, _):
        def far_block(b, _):
            attend(b, 2 * i)
            attend(b, 2 * i + 1)
            return 0

        lax.fori_loop(far_from, far_to, far_block, 0)
        even = o_acc[2 * i]
        odd = o_acc[2 * i + 1]
        even = pltpu.roll(even, HEAD_DIM, 1) / (even + sink_exp[pl.ds(2 * i, 1), :])
        odd = odd / (pltpu.roll(odd, HEAD_DIM, 1) + sink_exp[pl.ds(2 * i + 1, 1), :])
        ctx[t, i] = jnp.where(low, even, odd).astype(BF16)
        for dt in range(1, NT):
            ctx_copy(i, dt).start()
        return 0

    lax.fori_loop(0, PAIRS, finish_pair, 0)

    for dx in offsets:
        gather_o.along_other(dx).wait_recv()
        gather_o.twin_other(dx).start()
    for dx in range(NX):
        gather_o.twin_near(dx).wait_recv()
        gather_o.twin_other(dx).wait_recv()

    def project(tt):
        heads = jnp.concatenate([ctx[tt, i] for i in range(PAIRS)], axis=1)
        rows = wo_all[pl.ds(tt * (R // NT), R // NT)].reshape(WIDE, out.shape[1])
        return jnp.dot(heads, rows, preferred_element_type=F32)

    out_acc[...] = project(t)
    for dt in range(1, NT):
        for i in range(PAIRS):
            ctx_copy(i, dt).wait_recv()
        out_acc[...] += project(lax.rem(t + NT - dt, NT))
    out[...] = out_acc[...].astype(BF16)

    for gather in (gather_w, gather_o):
        gather.across().wait_send()
        for dx in offsets:
            gather.along(dx).wait_send()
            gather.along_other(dx).wait_send()
        for dx in range(NX):
            gather.twin_near(dx).wait_send()
            gather.twin_other(dx).wait_send()

    @pl.when(yh == 0)
    def _():
        gather_k.across().wait_send()

    for dx in offsets:
        gather_k.along(dx).wait_send()
    for dx in range(NX):
        gather_k.twin_near(dx).wait_send()

    @pl.when(yh == 1)
    def _():
        for dx in offsets:
            gather_k.along_other(dx).wait_send()
        for dx in range(NX):
            gather_k.twin_other(dx).wait_send()

    def sent(s, _):
        for d in range(2):
            for j in range(CHUNKS):
                ring(d, s, j).wait_send()

            @pl.when(s >= 1)
            def _():
                twin_plane(d, s).wait_send()

        return 0

    lax.fori_loop(0, H - 1, sent, 0)
    for d in range(2):
        twin_plane(d, H - 1).wait_send()
        for j in last_chunks(d):
            ring(d, H - 1, j).wait_send()
        twin_half(d).wait_send()

    def ctx_sent(i, _):
        for dt in range(1, NT):
            ctx_copy(i, dt).wait_send()
        return 0

    lax.fori_loop(0, PAIRS, ctx_sent, 0)


def spread_window(R):
    return -(-(15 * R + 127) // 128) * 128


def rotation_tables(rows, roles):
    half = HEAD_DIM // 2
    freq = np.exp(-math.log(150000.0) * np.arange(half) / half)
    freq = np.tile(freq, 128 // half)[None, :]
    near = np.arange(rows)[:, None] * freq
    far = (np.arange(roles) * rows)[:, None] * freq
    return [a.astype(np.float32) for a in (np.cos(near), np.sin(near), np.cos(far), np.sin(far))]


def on_device(sizes, tokens, gain, q_weight, kv_weight, out_weight, sinks, segments):
    NG, NT, R = sizes
    feature = tokens[0]
    docs = segments[0]
    rows, width = feature.shape
    NX = R // 4
    heads = q_weight.shape[1] // HEAD_DIM
    features_out = out_weight.shape[1]
    both = jnp.concatenate([q_weight, kv_weight], axis=1)
    w_in = jnp.pad(both, ((0, 1), (0, 0)))
    seg_rows = jnp.pad(docs.astype(BF16).reshape(rows // 128, 128), ((0, 16 - rows // 128), (0, 0)))
    seg_cols = jnp.broadcast_to(docs.astype(BF16)[:, None], (rows, 128))
    sink_exp = jnp.broadcast_to(jnp.exp(sinks)[:, None], (heads, 128))
    tables = [jnp.asarray(a) for a in rotation_tables(rows, R)]
    window = spread_window(R)
    norm_width = ((NG - 1) * 15 * R // 128) * 128 + window
    H = NG // 2
    dims = (NG, NT, R, NX, rows, width)
    vmem = pl.BlockSpec(memory_space=pltpu.VMEM)
    dma = pltpu.SemaphoreType.DMA
    out = pl.pallas_call(
        functools.partial(kernel, dims),
        out_shape=jax.ShapeDtypeStruct((rows, features_out), BF16),
        in_specs=[vmem] * 11,
        out_specs=vmem,
        scratch_shapes=[
            pltpu.VMEM((rows, norm_width), BF16),
            pltpu.VMEM((NG, rows, R * 16), BF16),
            pltpu.VMEM((NG, R, 16, both.shape[1]), BF16),
            pltpu.VMEM((rows, both.shape[1]), F32),
            pltpu.VMEM((heads, rows, 128), BF16),
            pltpu.VMEM((R, rows + 16, 128), BF16),
            pltpu.VMEM((R, rows, rows), F32),
            pltpu.VMEM((heads, rows, 128), F32),
            pltpu.VMEM((R, out_weight.shape[0], features_out), BF16),
            pltpu.VMEM((NT, heads // 2, rows, 128), BF16),
            pltpu.VMEM((rows, features_out), F32),
            dma((3, 4 * NX)),
            dma((3, 4 * NX)),
            dma((2, H, CHUNKS)),
            dma((2, H, CHUNKS)),
            dma((2, H + 1)),
            dma((2, H + 1)),
            dma((heads // 2, NT)),
            dma((heads // 2, NT)),
        ],
        compiler_params=pltpu.CompilerParams(collective_id=0, has_side_effects=True),
        name="layer",
    )(feature, gain[None], w_in, out_weight, seg_rows, seg_cols, sink_exp, *tables)
    return out[None]


def solution(mesh):
    placed = (
        P("group", "role", None),
        P(),
        P(("group", "role"), "tensor"),
        P(("group", "role"), "tensor"),
        P("role", "tensor"),
        P("tensor"),
        P("group", "role"),
    )
    sizes = (mesh.shape["group"], mesh.shape["tensor"], mesh.shape["role"])
    return jax.shard_map(
        functools.partial(on_device, sizes),
        mesh=mesh,
        in_specs=placed,
        out_specs=P("group", "role", "tensor"),
        check_vma=False,
    )
```

time: 328 us -> 116 us (0.35)
  the two profiles are of different devices: /device:TPU:60 before, /device:TPU:62 now
where the time goes in v1:
time: 116 us; the launch traced here: 115 us
  Pallas kernels  103 us (89%)
  local copies, waits for them, and re-layouts  10.1 us (9%)
  other arithmetic  2.03 us (2%)
    pallas_call x1, Pallas kernels, on_device(): pl.pallas_call(functools.partial(kernel, dims), out_shape=jax.ShapeDtypeS...  103 us
    unnamed x2, local copies, waits for them, and re-layouts  4.3 us

profile of v1, /device:TPU:62, one launch (start us, length us, event | category | flops | bytes accessed | tf_op | source)
XLA Modules:
  0.0 115.5 jit_solution(9250774067702145298)
XLA Ops:
  0.0 0.7 convert_reduce_fusion
  0.7 0.7 exp.3
  1.4 0.7 broadcast_in_dim.20.sink_exp
  2.0 0.6 pad.9.seg_rows
  2.6 1.3 %broadcast_in_dim.8.gain = f32[1,2880]{1,0:T(1,128)} reshape(f32[2880]{0:T(1024)} %param.12) | data formatting | bytes 23040 | tf_op jit(solution)/shard_map/broadcast_in_dim | solution.py:561
  3.9 1.3 %fusion.2.w_in = bf16[16,640]{1,0:T(8,128)(2,1)} fusion(bf16[15,128]{1,0:T(8,128)(2,1)} %param.14, bf16[15,512]{1,0:T(8,128)(2,1)} %param.13), kind=kLoop, calls=%fused_computation.3 | loop fusion | flops 71680 | bytes 39680 | tf_op jit(solution)/shard_map/concatenate | solution.py:521
  5.3 0.7 broadcast_in_dim.9.seg_cols
  6.0 1.7 %copy.13.wo_in = bf16[128,720]{1,0:T(8,128)(2,1)} copy(bf16[128,720]{0,1:T(8,128)(2,1)} %param.15) | data formatting | bytes 368640 | tf_op args[4]
  7.7 2.6 %copy.12 = bf16[1,256,2880]{2,1,0:T(8,128)(2,1)} copy(bf16[1,256,2880]{1,2,0:T(8,128)(2,1)} %param.11) | data formatting | bytes 2949120 | tf_op args[0]
  10.3 103.3 %layer.1 = bf16[256,720]{1,0:T(8,128)(2,1)} custom-call(bf16[256,2880]{1,0:T(8,128)(2,1)} %bitcast.3, f32[1,2880]{1,0:T(1,128)} %broadcast_in_dim.8.gain, bf16[16,640]{1,0:T(8,128)(2,1)} %fusion.2.w_in, bf16[128,720]{1,0:T(8,128)(2,1)} %copy.13.wo_in, bf16[16,128]{1,0:T(8,128)(2,1)} %pad.9.seg_rows, bf16[256,128]{1,0:T(8,128)(2,1)} %broadcast_in_dim.9.seg_cols, ...), custom_call_target="tpu_custom_call" | custom-call | tf_op jit(solution)/shard_map/layer/pallas_call | solution.py:533
  113.6 1.9 %copy.14 = bf16[1,256,720]{1,2,0:T(8,128)(2,1)} copy(bf16[1,256,720]{2,1,0:T(8,128)(2,1)} %bitcast.4) | data formatting | bytes 737280 | tf_op jit(solution)/shard_map/broadcast_in_dim | solution.py:562

commit v2 on v1

v2 whole, which is shorter than its diff:
```python
import functools
import math

import jax
import jax.numpy as jnp
import numpy as np
from jax import lax
from jax.experimental import pallas as pl
from jax.experimental.pallas import tpu as pltpu
from jax.sharding import PartitionSpec as P

HEAD_DIM = 64
REACH = 9
NEG = -1e30
LOG2E = 1.4426950408889634
F32 = jnp.float32
BF16 = jnp.bfloat16


def kernel(
    dims,
    tokens_hbm,
    gain,
    wq_in,
    wkv_in,
    wo_hbm,
    docs_in,
    sinks,
    near_cos,
    near_sin,
    far_cos,
    far_sin,
    out,
    tokens,
    normed,
    spread,
    w_own,
    w_all,
    acc,
    q_all,
    kv_all,
    v_all,
    docs_col,
    bias,
    o_acc,
    wo_all,
    ctx,
    out_acc,
    load_sem,
    plane_send,
    plane_recv,
    ring_send,
    ring_recv,
    side_send,
    side_recv,
    twin_send,
    twin_recv,
    ctx_send,
    ctx_recv,
    pass_send,
):
    NG, NT, R, NX, ROWS, D = dims
    HALF = R // 2
    H = NG // 2
    PAIRS = q_all.shape[0] // 2
    WIDE = q_all.shape[0] * HEAD_DIM
    g = lax.axis_index("group")
    t = lax.axis_index("tensor")
    r = lax.axis_index("role")
    c = lax.rem(r, 2)
    x = lax.rem(r // 2, NX)
    yh = r // HALF

    def role_of(y_, x_, c_):
        return y_ * HALF + x_ * 2 + c_

    def x_at(dx):
        return lax.rem(x + dx, NX)

    twin = {"role": role_of(yh, x, 1 - c)}
    across = {"role": role_of(1 - yh, x, c)}

    beyond = {"role": role_of(1 - yh, x_at(NX // 2), c)}

    def x_to(dx):
        return {"role": role_of(yh, x_at(dx), c)}

    up = lax.rem(g + 1, NG)
    down = lax.rem(g + NG - 1, NG)

    def remote(src, dst, send, recv, where):
        return pltpu.make_async_remote_copy(
            src_ref=src,
            dst_ref=dst,
            send_sem=send,
            recv_sem=recv,
            device_id=where,
            device_id_type=pl.DeviceIdType.MESH,
        )

    load_tokens = pltpu.make_async_copy(tokens_hbm, tokens, load_sem.at[0])
    load_tokens.start()
    load_wo = pltpu.make_async_copy(wo_hbm, wo_all.at[r], load_sem.at[1])
    load_wo.start()
    w_own[0:15, 0:WIDE] = wq_in[...]
    w_own[0:15, WIDE : WIDE + 128] = wkv_in[...]
    w_own[15:16, :] = jnp.zeros((1, WIDE + 128), BF16)

    greeted = [twin, across, {"group": up}, {"group": down}]
    greeted += [x_to(dx) for dx in range(1, NX)]
    if NX > 2:
        greeted += [beyond]
    greeted += [{"tensor": lax.rem(t + dt, NT)} for dt in range(1, NT)]
    barrier = pltpu.get_barrier_semaphore()
    for where in greeted:
        pl.semaphore_signal(
            barrier, inc=1, device_id=where, device_id_type=pl.DeviceIdType.MESH
        )
    pl.semaphore_wait(barrier, len(greeted))

    class Gather:
        def __init__(self, which, own, slot):
            self.send = plane_send.at[which]
            self.recv = plane_recv.at[which]
            self.own = own
            self.slot = slot

        def copy(self, index, role, where, src=None):
            dst = self.slot(role)
            return remote(
                dst if src is None else src, dst, self.send.at[index], self.recv.at[index], where
            )

        def across(self):
            return self.copy(0, r, across, self.own)

        def along(self, dx):
            return self.copy(dx, r, x_to(dx), self.own)

        def along_other(self, dx):
            return self.copy(NX - 1 + dx, role_of(1 - yh, x, c), x_to(dx))

        def twin_near(self, dx):
            if dx == 0:
                return self.copy(2 * NX, r, twin, self.own)
            return self.copy(2 * NX + dx, role_of(yh, lax.rem(x + NX - dx, NX), c), twin)

        def twin_other(self, dx):
            return self.copy(3 * NX + dx, role_of(1 - yh, lax.rem(x + NX - dx, NX), c), twin)

    gather_k = Gather(2, kv_all.at[r], lambda role: kv_all.at[role])
    offsets = range(1, NX)

    far = [2] if NX > 2 else []
    near = [1, NX - 1] if NX > 2 else [1]
    upper = (wo_all.shape[1] // 2) // 16 * 16

    def own_block(slot):
        return w_all.at[g, c * HALF + slot]

    def w_copy(index, slot, where):
        return remote(
            w_own, own_block(slot), plane_send.at[0, index], plane_recv.at[0, index], where
        )

    w_across = w_copy(0, NX, across)
    w_far = [w_copy(1, dx, x_to(dx)) for dx in far]
    w_beyond = [w_copy(2, NX + dx, beyond) for dx in far]
    travels = {0: 0, NX: 2}
    for dx in far:
        travels.update({dx: 1, NX + dx: 2})

    def plane(d, s):
        return lax.rem(g - s + NG, NG) if d == 0 else lax.rem(g + s, NG)

    def ring(d, s, j):
        dst = w_all.at[plane(d, s), c * HALF + j]
        return remote(
            w_own if s == 0 and j == 0 else dst,
            dst,
            ring_send.at[d, s, j],
            ring_recv.at[d, s, j],
            {"group": up if d == 0 else down},
        )

    def side(d, s, j, i):
        slot = c * HALF + j
        index = (d, s, 2 * (j // NX) + i)
        return remote(
            w_own if s == 0 and j == 0 else w_all.at[plane(d, s), slot],
            w_all.at[plane(d, s), slot + near[i]],
            side_send.at[index],
            side_recv.at[index],
            x_to(near[i]),
        )

    def sides(d, s):
        return [side(d, s, j, i) for j in (0, NX) for i in range(len(near))]

    def both(s):
        return range(2 if 0 < s < H else 1)

    def o_copy(index, role, where, rows=None):
        ref = wo_all.at[role] if rows is None else wo_all.at[role, rows]
        return remote(ref, ref, plane_send.at[1, index], plane_recv.at[1, index], where)

    def behind(y_, dx):
        return role_of(y_, lax.rem(x + NX - dx, NX), c)

    def halves():
        return (pl.ds(0, upper), pl.ds(upper, wo_all.shape[1] - upper))

    o_across = o_copy(0, r, across)

    def o_side(dy, i):
        return o_copy(1 + 4 * dy + i, behind(yh if dy == 0 else 1 - yh, 0), x_to(near[i]))

    def o_on(dy, i):
        role = behind(yh if dy == 0 else 1 - yh, near[i])
        return o_copy(3 + 4 * dy + i, role, x_to(near[i]), halves()[i])

    def o_twin(dy, dx):
        return o_copy(9 + dy * NX + dx, behind(yh if dy == 0 else 1 - yh, dx), twin)

    def o_take_sides(dy):
        for i in range(len(near)):
            o_side(dy, i).wait_recv()
            if far:
                o_on(dy, i).start()
            o_twin(dy, near[i]).start()

    def o_take_far(dy):
        for dx in far:
            for i in range(2):
                o_on(dy, i).wait_recv()
            o_twin(dy, dx).start()

    def twin_plane(d, s):
        ref = w_all.at[plane(d, s), pl.ds(c * HALF, HALF)]
        return remote(ref, ref, twin_send.at[d, s], twin_recv.at[d, s], twin)

    def last(j):
        return j // NX

    def add_plane(p):
        acc[...] += jnp.dot(
            spread[p],
            w_all[p].reshape(R * 16, acc.shape[1]),
            preferred_element_type=F32,
        )

    def round_of_ring(n):
        for j, delay in travels.items():
            s = n - delay
            if s < 0 or s > H:
                continue
            if s == 0 and j == NX:
                w_across.wait_recv()
            elif s == 0 and j > NX:
                w_beyond[0].wait_recv()
            elif s == 0 and j > 0:
                w_far[0].wait_recv()
            for d in range(2):
                if 1 <= s < H or (s == H and d == last(j)):
                    ring(d, s - 1, j).wait_recv()
                if s < H - 1 or (s == H - 1 and d == last(j)):
                    ring(d, s, j).start()
            if j % NX == 0:
                for d in both(s):
                    for i in range(len(near)):
                        side(d, s, j, i).start()
        whole = n - 3
        if whole >= 0:
            for d in both(whole):
                for copy in sides(d, whole):
                    copy.wait_recv()
                twin_plane(d, whole).start()

    def add_planes(s):
        for d in both(s):
            twin_plane(d, s).wait_recv()
            add_plane(plane(d, s))

    w_across.start()
    for copy in w_beyond + w_far:
        copy.start()
    round_of_ring(0)
    w_all[g, c * HALF] = w_own[...]
    load_wo.wait()
    o_across.start()
    for i in range(len(near)):
        o_side(0, i).start()
    o_twin(0, 0).start()

    load_tokens.wait()

    def add_squares(i, total):
        wide = tokens[pl.ds(pl.multiple_of(i * 160, 32), 160), :].astype(F32)
        return total + jnp.sum((wide * wide).reshape(20, 8, ROWS), axis=0)

    squares = lax.fori_loop(0, D // 160, add_squares, jnp.zeros((8, ROWS), F32))
    scale = lax.rsqrt(jnp.sum(squares, axis=0, keepdims=True) * (1.0 / D) + 1e-05)

    def norm_rows(start, count):
        row = jnp.broadcast_to(gain[pl.ds(start, count)][None], (128, count))
        column = jnp.transpose(row)
        wide = tokens[pl.ds(start, count), :].astype(F32)
        normed[pl.ds(start, count), :] = (
            wide * scale * jnp.concatenate([column] * (ROWS // 128), axis=1)
        ).astype(BF16)

    def norm_full(i, _):
        norm_rows(pl.multiple_of(i * 128, 128), 128)
        return 0

    lax.fori_loop(0, D // 128, norm_full, 0)
    if D % 128:
        norm_rows(D // 128 * 128, D % 128)
    round_of_ring(1)
    round_of_ring(2)
    lane = lax.broadcasted_iota(jnp.int32, (15 * R, R * 16), 1)
    slot_of = lane // 16
    within = lax.rem(lane, 16)
    rel = lax.rem(slot_of, HALF)
    slot_role = role_of(
        lax.rem(yh + rel // NX, 2), lax.rem(x + NX - lax.rem(rel, NX), NX), slot_of // HALF
    )
    feature = jnp.where(within < 15, slot_role * 15 + within, -1)
    hit = lax.broadcasted_iota(jnp.int32, (15 * R, R * 16), 0) == feature
    pick = jnp.where(hit, 1.0, 0.0).astype(BF16)

    def spread_plane(p, _):
        part = normed[pl.ds(pl.multiple_of(p * (15 * R), 8), 15 * R), :]
        spread[p] = lax.dot_general(
            part, pick, (((0,), (0,)), ((), ())), preferred_element_type=F32
        ).astype(BF16)
        return 0

    lax.fori_loop(0, NG, spread_plane, 0)
    acc[...] = jnp.zeros_like(acc)
    docs = docs_in[...].astype(F32)
    for part in range(ROWS // 128):
        row = jnp.broadcast_to(docs[:, 128 * part : 128 * (part + 1)], (128, 128))
        docs_col[128 * part : 128 * (part + 1), :] = jnp.transpose(row)
    round_of_ring(3)
    for n in range(4, H + 4):
        round_of_ring(n)
        add_planes(n - 4)
        if n == 5:
            o_take_sides(0)
    add_planes(H)

    cos_far = far_cos[pl.ds(r, 1), :]
    sin_far = far_sin[pl.ds(r, 1), :]
    cos = near_cos[...] * cos_far - near_sin[...] * sin_far
    sin = near_sin[...] * cos_far + near_cos[...] * sin_far
    lanes = lax.broadcasted_iota(jnp.int32, (ROWS, 128), 1)
    first_half = lax.rem(lanes, HEAD_DIM) < HEAD_DIM // 2
    low = lanes < HEAD_DIM
    signed = jnp.where(first_half, -sin, sin)

    def swapped(u):
        return jnp.where(
            first_half, pltpu.roll(u, 128 - HEAD_DIM // 2, 1), pltpu.roll(u, HEAD_DIM // 2, 1)
        )

    pair = acc[:, WIDE : WIDE + 128]
    turned = pair * jnp.where(low, cos, 1.0) + swapped(pair) * jnp.where(low, signed, 0.0)
    kv_all[r, 0:ROWS] = turned.astype(BF16)
    doc_rows = jnp.zeros((16, 128), F32)
    line = lax.broadcasted_iota(jnp.int32, (16, 128), 0)
    for part in range(ROWS // 128):
        doc_rows = jnp.where(line == part, docs[:, 128 * part : 128 * (part + 1)], doc_rows)
    kv_all[r, ROWS : ROWS + 16] = doc_rows.astype(BF16)

    @pl.when(yh == 0)
    def _():
        gather_k.across().start()

    for dx in offsets:
        gather_k.along(dx).start()
    gather_k.twin_near(0).start()
    o_across.wait_recv()
    for i in range(len(near)):
        o_side(1, i).start()
    o_twin(1, 0).start()

    fold = 0.125 * LOG2E
    for i in range(PAIRS):
        u = acc[:, 128 * i : 128 * (i + 1)]
        turned = (u * cos + swapped(u) * signed) * fold
        q_all[2 * i] = jnp.where(low, turned, 0.0).astype(BF16)
        q_all[2 * i + 1] = jnp.where(low, pltpu.roll(turned, HEAD_DIM, 1), 0.0).astype(BF16)

    q_pos = lax.broadcasted_iota(jnp.int32, (ROWS, 128), 0) + r * ROWS
    k_off = lax.broadcasted_iota(jnp.int32, (ROWS, 128), 1)

    def make_bias(b):
        for part in range(ROWS // 128):
            keys = kv_all[b, ROWS + part : ROWS + part + 1, :].astype(F32)
            seen = (docs_col[...] == keys) & (k_off + (b * ROWS + part * 128) <= q_pos)
            bias[b, :, part * 128 : (part + 1) * 128] = jnp.where(seen, 0.0, NEG)
        block = kv_all[b, 0:ROWS, :]
        v_all[b] = jnp.where(low, 1.0, block.astype(F32)).astype(BF16)

    def attend(b, h, count, fresh=False):
        heads = pl.ds(h, count)
        scores = lax.dot_general(
            q_all[heads].reshape(count * ROWS, 128),
            kv_all[b, 0:ROWS, :],
            (((1,), (1,)), ((), ())),
            preferred_element_type=F32,
        )
        weights = jnp.exp2(scores.reshape(count, ROWS, ROWS) + bias[b][None]).astype(BF16)
        added = jnp.dot(
            weights.reshape(count * ROWS, ROWS), v_all[b], preferred_element_type=F32
        ).reshape(count, ROWS, 128)
        if fresh:
            o_acc[heads] = added
        else:
            o_acc[heads] += added

    STACK = PAIRS

    make_bias(r)

    attend(r, 0, STACK, True)
    attend(r, STACK, STACK, True)

    for dx in offsets:
        gather_k.along(dx).wait_recv()
        gather_k.twin_near(dx).start()

    @pl.when(yh == 1)
    def _():
        gather_k.across().wait_recv()
        for dx in offsets:
            gather_k.along_other(dx).start()
        gather_k.twin_other(0).start()

    for dx in range(NX):
        gather_k.twin_near(dx).wait_recv()

    def near_block(b, _):
        make_bias(b)
        attend(b, 0, STACK)
        attend(b, STACK, STACK)
        return 0

    lax.fori_loop(yh * HALF, r, near_block, 0)

    @pl.when(yh == 1)
    def _():
        for dx in offsets:
            gather_k.along_other(dx).wait_recv()
            gather_k.twin_other(dx).start()

    o_take_far(0)
    o_take_sides(1)

    far_from = jnp.maximum(r - REACH, 0)
    far_to = jnp.where(yh == 1, HALF, far_from)

    @pl.when(yh == 1)
    def _():
        for dx in range(NX):
            gather_k.twin_other(dx).wait_recv()

        def far_bias(b, _):
            make_bias(b)
            return 0

        lax.fori_loop(far_from, HALF, far_bias, 0)

    def sink_of(h):
        return jnp.exp(jnp.full((1, 128), sinks[h], F32))

    def ctx_copy(i, dt):
        ref = ctx.at[t, i]
        return remote(
            ref, ref, ctx_send.at[i, dt], ctx_recv.at[i, dt], {"tensor": lax.rem(t + dt, NT)}
        )

    ends = NT == 4

    def direct(dt):
        if not ends:
            return t >= 0
        return jnp.abs(lax.rem(t + dt, NT) - t) < 3

    def ctx_pass(i, dt):
        ref = ctx.at[lax.rem(t + 2, NT), i]
        return remote(
            ref,
            ref,
            pass_send.at[i],
            ctx_recv.at[i, dt],
            {"tensor": lax.rem(t + dt + 2, NT)},
        )

    def finish_stack(k, _):
        def far_block(b, _):
            attend(b, STACK * k, STACK)
            return 0

        lax.fori_loop(far_from, far_to, far_block, 0)
        for n in range(STACK // 2):
            i = k * (STACK // 2) + n
            even = o_acc[2 * i]
            odd = o_acc[2 * i + 1]
            even = pltpu.roll(even, HEAD_DIM, 1) / (even + sink_of(2 * i))
            odd = odd / (pltpu.roll(odd, HEAD_DIM, 1) + sink_of(2 * i + 1))
            ctx[t, i] = jnp.where(low, even, odd).astype(BF16)
            for dt in range(1, NT):

                @pl.when(direct(dt))
                def _(i=i, dt=dt):
                    ctx_copy(i, dt).start()

        return 0

    lax.fori_loop(0, 2, finish_stack, 0)

    def project(tt):
        total = None
        for i in range(0, PAIRS, 2):
            role = tt * (R // NT) + i
            rows = jnp.concatenate([wo_all[role], wo_all[role + 1]], axis=1)
            heads = jnp.concatenate([ctx[tt, i], ctx[tt, i + 1]], axis=1)
            part = lax.dot_general(
                rows, heads, (((1,), (1,)), ((), ())), preferred_element_type=F32
            )
            total = part if total is None else total + part
        return total

    if ends:
        for where, dt in ((1, 1), (2, 3)):

            @pl.when(t == where)
            def _(dt=dt):
                for i in range(PAIRS):
                    ctx_copy(i, 2).wait_recv()
                    ctx_pass(i, dt).start()

    o_take_far(1)
    for dy in range(2):
        for dx in range(NX):
            o_twin(dy, dx).wait_recv()
    out_acc[...] = project(t)
    order = (1, 3, 2) if ends else tuple(range(1, NT))
    for dt in order:
        if ends and dt == 2:

            @pl.when((t == 0) | (t == 3))
            def _():
                for i in range(PAIRS):
                    ctx_copy(i, dt).wait_recv()
        else:
            for i in range(PAIRS):
                ctx_copy(i, dt).wait_recv()
        out_acc[...] += project(lax.rem(t + NT - dt, NT))
    out[...] = out_acc[...].astype(BF16)

    for copy in [w_across, o_across] + w_far + w_beyond:
        copy.wait_send()
    for dy in range(2):
        for i in range(len(near)):
            o_side(dy, i).wait_send()
            if far:
                o_on(dy, i).wait_send()
        for dx in range(NX):
            o_twin(dy, dx).wait_send()

    @pl.when(yh == 0)
    def _():
        gather_k.across().wait_send()

    for dx in offsets:
        gather_k.along(dx).wait_send()
    for dx in range(NX):
        gather_k.twin_near(dx).wait_send()

    @pl.when(yh == 1)
    def _():
        for dx in offsets:
            gather_k.along_other(dx).wait_send()
        for dx in range(NX):
            gather_k.twin_other(dx).wait_send()

    for j in travels:
        for s in range(H):
            for d in range(2):
                if s < H - 1 or d == last(j):
                    ring(d, s, j).wait_send()
    for s in range(H + 1):
        for d in both(s):
            for copy in sides(d, s) + [twin_plane(d, s)]:
                copy.wait_send()
    for i in range(PAIRS):
        for dt in range(1, NT):

            @pl.when(direct(dt))
            def _(i=i, dt=dt):
                ctx_copy(i, dt).wait_send()

    if ends:

        @pl.when((t == 1) | (t == 2))
        def _():
            for i in range(PAIRS):
                ctx_pass(i, 1).wait_send()


def rotation_tables(rows, roles):
    half = HEAD_DIM // 2
    freq = np.exp(-math.log(150000.0) * np.arange(half) / half)
    freq = np.tile(freq, 128 // half)[None, :]
    near = np.arange(rows)[:, None] * freq
    far = (np.arange(roles) * rows)[:, None] * freq
    return [a.astype(np.float32) for a in (np.cos(near), np.sin(near), np.cos(far), np.sin(far))]


def on_device(sizes, tokens, gain, q_weight, kv_weight, out_weight, sinks, segments):
    NG, NT, R = sizes
    feature = tokens[0].T
    width, rows = feature.shape
    NX = R // 4
    heads = q_weight.shape[1] // HEAD_DIM
    columns = q_weight.shape[1] + kv_weight.shape[1]
    features_out = out_weight.shape[1]
    tables = [jnp.asarray(a) for a in rotation_tables(rows, R)]
    H = NG // 2
    dims = (NG, NT, R, NX, rows, width)
    vmem = pl.BlockSpec(memory_space=pltpu.VMEM)
    anywhere = pl.BlockSpec(memory_space=pl.ANY)
    dma = pltpu.SemaphoreType.DMA
    out = pl.pallas_call(
        functools.partial(kernel, dims),
        out_shape=jax.ShapeDtypeStruct((features_out, rows), BF16),
        in_specs=[anywhere, vmem, vmem, vmem, anywhere, vmem]
        + [pl.BlockSpec(memory_space=pltpu.SMEM)]
        + [vmem] * 4,
        out_specs=vmem,
        scratch_shapes=[
            pltpu.VMEM((width, rows), BF16),
            pltpu.VMEM((width, rows), BF16),
            pltpu.VMEM((NG, rows, R * 16), BF16),
            pltpu.VMEM((16, columns), BF16),
            pltpu.VMEM((NG, R, 16, columns), BF16),
            pltpu.VMEM((rows, columns), F32),
            pltpu.VMEM((heads, rows, 128), BF16),
            pltpu.VMEM((R, rows + 16, 128), BF16),
            pltpu.VMEM((R, rows, 128), BF16),
            pltpu.VMEM((rows, 128), F32),
            pltpu.VMEM((R, rows, rows), F32),
            pltpu.VMEM((heads, rows, 128), F32),
            pltpu.VMEM((R, features_out, 128), BF16),
            pltpu.VMEM((NT, heads // 2, rows, 128), BF16),
            pltpu.VMEM((features_out, rows), F32),
            dma((2,)),
            dma((3, 9 + 2 * NX)),
            dma((3, 9 + 2 * NX)),
            dma((2, H, R // 2)),
            dma((2, H, R // 2)),
            dma((2, H + 1, 4)),
            dma((2, H + 1, 4)),
            dma((2, H + 1)),
            dma((2, H + 1)),
            dma((heads // 2, NT)),
            dma((heads // 2, NT)),
            dma((heads // 2,)),
        ],
        compiler_params=pltpu.CompilerParams(collective_id=0, has_side_effects=True),
        name="layer",
    )(
        feature,
        gain,
        q_weight,
        kv_weight,
        out_weight.T,
        segments,
        sinks,
        *tables,
    )
    return out.T[None]


def solution(mesh):
    placed = (
        P("group", "role", None),
        P(),
        P(("group", "role"), "tensor"),
        P(("group", "role"), "tensor"),
        P("role", "tensor"),
        P("tensor"),
        P("group", "role"),
    )
    sizes = (mesh.shape["group"], mesh.shape["tensor"], mesh.shape["role"])
    return jax.shard_map(
        functools.partial(on_device, sizes),
        mesh=mesh,
        in_specs=placed,
        out_specs=P("group", "role", "tensor"),
        check_vma=False,
    )
```

time: 116 us -> 97.8 us (0.84)
  the two profiles are of different devices: /device:TPU:62 before, /device:TPU:57 now
where the time goes in v2:
time: 97.8 us; the launch traced here: 97.7 us
  Pallas kernels  95.9 us (98%)
  local copies, waits for them, and re-layouts  1.75 us (2%)
    pallas_call x1, Pallas kernels, on_device(): pl.pallas_call(functools.partial(kernel, dims), out_shape=jax.ShapeDtypeS...  95.9 us

profile of v2, /device:TPU:57, one launch (start us, length us, event | category | flops | bytes accessed | tf_op | source)
XLA Modules:
  0.0 97.7 jit_solution(2145988813793067284)
XLA Ops:
  0.0 95.9 %layer.1 = bf16[720,256]{1,0:T(8,128)(2,1)} custom-call(bf16[2880,256]{1,0:T(8,128)(2,1)} %bitcast.8, f32[2880]{0:T(1024)} %gain.1, bf16[15,512]{1,0:T(8,128)(2,1)} %wq_in.1, bf16[15,128]{1,0:T(8,128)(2,1)} %wkv_in.1, bf16[720,128]{1,0:T(8,128)(2,1)} %bitcast.9, s32[1,256]{1,0:T(1,128)} %docs_in.1, f32[8]{0:T(128)} %sinks.1, ...), custom_call_target="tpu_custom_call" | custom-call | tf_op jit(solution)/shard_map/layer/pallas_call | solution.py:637
  95.9 1.7 %copy.13 = bf16[1,256,720]{1,2,0:T(8,128)(2,1)} copy(bf16[1,256,720]{1,2,0:T(8,128)(2,1)} %bitcast.7) | data formatting | bytes 737280

commit v3 on v2

--- a/solution.py
+++ b/solution.py
@@ -45,6 +45,7 @@
     o_acc,
     wo_all,
     ctx,
+    around,
     out_acc,
     load_sem,
     plane_send,
@@ -58,6 +59,8 @@
     ctx_send,
     ctx_recv,
     pass_send,
+    around_send,
+    around_recv,
 ):
     NG, NT, R, NX, ROWS, D = dims
     HALF = R // 2
@@ -85,8 +88,9 @@
     def x_to(dx):
         return {"role": role_of(yh, x_at(dx), c)}
 
-    up = lax.rem(g + 1, NG)
-    down = lax.rem(g + NG - 1, NG)
+    def along_ring(d, hop):
+        return {"group": lax.rem(g + hop, NG) if d == 0 else lax.rem(g + NG - hop, NG)}
+
 
     def remote(src, dst, send, recv, where):
         return pltpu.make_async_remote_copy(
@@ -106,10 +110,18 @@
     w_own[0:15, WIDE : WIDE + 128] = wkv_in[...]
     w_own[15:16, :] = jnp.zeros((1, WIDE + 128), BF16)
 
-    greeted = [twin, across, {"group": up}, {"group": down}]
+    greeted = [twin, across] + [along_ring(d, hop) for d in range(2) for hop in (1, 2)]
     greeted += [x_to(dx) for dx in range(1, NX)]
     if NX > 2:
         greeted += [beyond]
+    ends = NT == 4
+    middle = (t == 1) | (t == 2)
+    if ends:
+        other = role_of(1 - yh, x, c)
+        greeted += [
+            {"tensor": jnp.where(middle, 0, 1), "role": other},
+            {"tensor": jnp.where(middle, 3, 2), "role": other},
+        ]
     greeted += [{"tensor": lax.rem(t + dt, NT)} for dt in range(1, NT)]
     barrier = pltpu.get_barrier_semaphore()
     for where in greeted:
@@ -166,21 +178,22 @@
     w_across = w_copy(0, NX, across)
     w_far = [w_copy(1, dx, x_to(dx)) for dx in far]
     w_beyond = [w_copy(2, NX + dx, beyond) for dx in far]
-    travels = {0: 0, NX: 2}
+    travels = {0: 0.0, NX: 6.0}
     for dx in far:
-        travels.update({dx: 1, NX + dx: 2})
+        travels.update({dx: 3.0, NX + dx: 7.5})
 
     def plane(d, s):
         return lax.rem(g - s + NG, NG) if d == 0 else lax.rem(g + s, NG)
 
     def ring(d, s, j):
-        dst = w_all.at[plane(d, s), c * HALF + j]
+        hop = 2 if s % 2 == 0 else 1
+        dst = w_all.at[plane(d, s - hop), c * HALF + j]
         return remote(
-            w_own if s == 0 and j == 0 else dst,
+            w_own if s == hop and j == 0 else dst,
             dst,
-            ring_send.at[d, s, j],
-            ring_recv.at[d, s, j],
-            {"group": up if d == 0 else down},
+            ring_send.at[d, s - 1, j],
+            ring_recv.at[d, s - 1, j],
+            along_ring(d, hop),
         )
 
     def side(d, s, j, i):
@@ -249,32 +262,35 @@
             preferred_element_type=F32,
         )
 
-    def round_of_ring(n):
-        for j, delay in travels.items():
-            s = n - delay
-            if s < 0 or s > H:
-                continue
-            if s == 0 and j == NX:
-                w_across.wait_recv()
-            elif s == 0 and j > NX:
-                w_beyond[0].wait_recv()
-            elif s == 0 and j > 0:
-                w_far[0].wait_recv()
-            for d in range(2):
-                if 1 <= s < H or (s == H and d == last(j)):
-                    ring(d, s - 1, j).wait_recv()
-                if s < H - 1 or (s == H - 1 and d == last(j)):
-                    ring(d, s, j).start()
-            if j % NX == 0:
-                for d in both(s):
-                    for i in range(len(near)):
-                        side(d, s, j, i).start()
-        whole = n - 3
-        if whole >= 0:
-            for d in both(whole):
-                for copy in sides(d, whole):
-                    copy.wait_recv()
-                twin_plane(d, whole).start()
+    def ways(s, j):
+        return (last(j),) if s == H else (0, 1)
+
+    def onward(s, j):
+        return [s + hop for hop in (1, 2) if s % 2 == 0 and s + hop <= H]
+
+    def take(s, j):
+        if s == 0 and j == NX:
+            w_across.wait_recv()
+        elif s == 0 and j > NX:
+            w_beyond[0].wait_recv()
+        elif s == 0 and j > 0:
+            w_far[0].wait_recv()
+        for d in range(2):
+            if s > 0 and d in ways(s, j):
+                ring(d, s, j).wait_recv()
+            for to in onward(s, j)[::-1]:
+                if d in ways(to, j):
+                    ring(d, to, j).start()
+        if j % NX == 0:
+            for d in both(s):
+                for i in range(len(near)):
+                    side(d, s, j, i).start()
+
+    def share(s):
+        for d in both(s):
+            for copy in sides(d, s):
+                copy.wait_recv()
+            twin_plane(d, s).start()
 
     def add_planes(s):
         for d in both(s):
@@ -284,7 +300,7 @@
     w_across.start()
     for copy in w_beyond + w_far:
         copy.start()
-    round_of_ring(0)
+    take(0, 0)
     w_all[g, c * HALF] = w_own[...]
     load_wo.wait()
     o_across.start()
@@ -316,8 +332,6 @@
     lax.fori_loop(0, D // 128, norm_full, 0)
     if D % 128:
         norm_rows(D // 128 * 128, D % 128)
-    round_of_ring(1)
-    round_of_ring(2)
     lane = lax.broadcasted_iota(jnp.int32, (15 * R, R * 16), 1)
     slot_of = lane // 16
     within = lax.rem(lane, 16)
@@ -336,20 +350,32 @@
         ).astype(BF16)
         return 0
 
-    lax.fori_loop(0, NG, spread_plane, 0)
+    def spread_planes(part):
+        lax.fori_loop(part * (NG // 2), (part + 1) * (NG // 2), spread_plane, 0)
+
     acc[...] = jnp.zeros_like(acc)
     docs = docs_in[...].astype(F32)
     for part in range(ROWS // 128):
         row = jnp.broadcast_to(docs[:, 128 * part : 128 * (part + 1)], (128, 128))
         docs_col[128 * part : 128 * (part + 1), :] = jnp.transpose(row)
-    round_of_ring(3)
-    for n in range(4, H + 4):
-        round_of_ring(n)
-        add_planes(n - 4)
-        if n == 5:
-            o_take_sides(0)
-    add_planes(H)
-
+    STEP, SKIP = 3.4, 4.4
+
+    def due(s, j):
+        return travels[j] + (s // 2) * SKIP + (s % 2) * STEP
+
+    tasks = []
+    for s in range(H + 1):
+        for j in travels:
+            if s > 0 or j > 0:
+                tasks.append((due(s, j), functools.partial(take, s, j)))
+        there = max(max(due(s, j) for j in travels), max(due(s, 0), due(s, NX)) + STEP)
+        tasks.append((there, functools.partial(share, s)))
+        tasks.append((there + 4.0 if s <= H // 3 else 90.0 + s, functools.partial(add_planes, s)))
+    tasks.append((14.0, functools.partial(o_take_sides, 0)))
+    tasks.append((3.8, functools.partial(spread_planes, 0)))
+    tasks.append((8.2, functools.partial(spread_planes, 1)))
+    for _, task in sorted(tasks, key=lambda one: one[0]):
+        task()
     cos_far = far_cos[pl.ds(r, 1), :]
     sin_far = far_sin[pl.ds(r, 1), :]
     cos = near_cos[...] * cos_far - near_sin[...] * sin_far
@@ -447,7 +473,13 @@
         attend(b, STACK, STACK)
         return 0
 
-    lax.fori_loop(yh * HALF, r, near_block, 0)
+    lax.fori_loop(yh * HALF, jnp.where(yh == 1, r, 0), near_block, 0)
+
+    @pl.when(yh == 1)
+    def _():
+        gather_k.twin_other(0).wait_recv()
+        near_block(role_of(0, x, c), 0)
+        near_block(role_of(0, x, 1 - c), 0)
 
     @pl.when(yh == 1)
     def _():
@@ -459,18 +491,24 @@
     o_take_sides(1)
 
     far_from = jnp.maximum(r - REACH, 0)
-    far_to = jnp.where(yh == 1, HALF, far_from)
+    far_to = jnp.where(yh == 1, HALF, r)
 
     @pl.when(yh == 1)
     def _():
-        for dx in range(NX):
+        for dx in offsets:
             gather_k.twin_other(dx).wait_recv()
 
-        def far_bias(b, _):
+    def in_finish(b):
+        return (yh == 0) | (b // 2 != x)
+
+    def far_bias(b, _):
+        @pl.when(in_finish(b))
+        def _():
             make_bias(b)
-            return 0
-
-        lax.fori_loop(far_from, HALF, far_bias, 0)
+
+        return 0
+
+    lax.fori_loop(far_from, far_to, far_bias, 0)
 
     def sink_of(h):
         return jnp.exp(jnp.full((1, 128), sinks[h], F32))
@@ -481,26 +519,49 @@
             ref, ref, ctx_send.at[i, dt], ctx_recv.at[i, dt], {"tensor": lax.rem(t + dt, NT)}
         )
 
-    ends = NT == 4
-
     def direct(dt):
         if not ends:
             return t >= 0
-        return jnp.abs(lax.rem(t + dt, NT) - t) < 3
-
-    def ctx_pass(i, dt):
-        ref = ctx.at[lax.rem(t + 2, NT), i]
+        apart = jnp.abs(lax.rem(t + dt, NT) - t)
+        return (apart == 1) | ((apart == 2) & jnp.logical_not(middle))
+
+    to_end = jnp.where(t == 1, 0, 3)
+    turning = STACK // 2
+    rounds = x < NX // 2
+
+    def ctx_pass(i, kind):
+        source = 3 - t if kind == 0 else jnp.where(t == 1, 3, 0)
+        ref = ctx.at[source, i]
+        back = lax.rem(to_end + NT - source, NT)
         return remote(
-            ref,
-            ref,
-            pass_send.at[i],
-            ctx_recv.at[i, dt],
-            {"tensor": lax.rem(t + dt + 2, NT)},
+            ref, ref, pass_send.at[kind, i], ctx_recv.at[i, back], {"tensor": to_end}
+        )
+
+    def around_out(i):
+        return remote(
+            ctx.at[t, i],
+            around.at[i],
+            around_send.at[0, i],
+            around_recv.at[i],
+            {"tensor": jnp.where(t == 0, 2, 1), "role": role_of(0, x, c)},
+        )
+
+    def around_on(i):
+        source = jnp.where(t == 2, 0, 3)
+        return remote(
+            around.at[i],
+            ctx.at[source, i],
+            around_send.at[1, i],
+            ctx_recv.at[i, lax.rem(3 - source + NT - source, NT)],
+            {"tensor": 3 - source, "role": role_of(1, x, c)},
         )
 
     def finish_stack(k, _):
         def far_block(b, _):
-            attend(b, STACK * k, STACK)
+            @pl.when(in_finish(b))
+            def _():
+                attend(b, STACK * k, STACK)
+
             return 0
 
         lax.fori_loop(far_from, far_to, far_block, 0)
@@ -511,7 +572,13 @@
             even = pltpu.roll(even, HEAD_DIM, 1) / (even + sink_of(2 * i))
             odd = odd / (pltpu.roll(odd, HEAD_DIM, 1) + sink_of(2 * i + 1))
             ctx[t, i] = jnp.where(low, even, odd).astype(BF16)
-            for dt in range(1, NT):
+            if ends:
+
+                @pl.when((yh == 1) & rounds & jnp.logical_not(middle) & (k == 0))
+                def _(i=i):
+                    around_out(i).start()
+
+            for dt in (2, 1, 3)[: NT - 1] if ends else range(1, NT):
 
                 @pl.when(direct(dt))
                 def _(i=i, dt=dt):
@@ -534,31 +601,53 @@
         return total
 
     if ends:
-        for where, dt in ((1, 1), (2, 3)):
-
-            @pl.when(t == where)
-            def _(dt=dt):
-                for i in range(PAIRS):
-                    ctx_copy(i, 2).wait_recv()
-                    ctx_pass(i, dt).start()
+
+        @pl.when(middle)
+        def _():
+            def relay(i):
+                ctx_copy(i, 2).wait_recv()
+                ctx_pass(i, 1).start()
+
+            for i in range(PAIRS):
+                ctx_copy(i, jnp.where(t == 1, 3, 1)).wait_recv()
+                ctx_pass(i, 0).start()
+                if i >= turning:
+                    relay(i)
+                else:
+                    pl.when((yh == 0) | jnp.logical_not(rounds))(functools.partial(relay, i))
+
+            @pl.when((yh == 0) & rounds)
+            def _():
+                for i in range(turning):
+                    around_out(i).wait_recv()
+                    around_on(i).start()
 
     o_take_far(1)
     for dy in range(2):
         for dx in range(NX):
             o_twin(dy, dx).wait_recv()
     out_acc[...] = project(t)
-    order = (1, 3, 2) if ends else tuple(range(1, NT))
-    for dt in order:
-        if ends and dt == 2:
-
-            @pl.when((t == 0) | (t == 3))
-            def _():
-                for i in range(PAIRS):
-                    ctx_copy(i, dt).wait_recv()
-        else:
-            for i in range(PAIRS):
+    for k in range(1, NT):
+        source = lax.rem(t + k, NT)
+        if ends:
+            order = ((1, 2, 3), (0, 2, 3), (1, 3, 0), (2, 1, 0))
+            source = order[3][k - 1]
+            for where in range(3):
+                source = jnp.where(t == where, order[where][k - 1], source)
+        dt = lax.rem(t + NT - source, NT)
+        for i in range(PAIRS):
+            waited = (t < 0) | (t > NT)
+            if ends:
+                passed = dt == 2
+                if i < turning:
+                    passed = passed & ((yh == 0) | jnp.logical_not(rounds))
+                waited = middle & ((source == 1) | (source == 2) | passed)
+
+            @pl.when(jnp.logical_not(waited))
+            def _(i=i, dt=dt):
                 ctx_copy(i, dt).wait_recv()
-        out_acc[...] += project(lax.rem(t + NT - dt, NT))
+
+        out_acc[...] += project(source)
     out[...] = out_acc[...].astype(BF16)
 
     for copy in [w_across, o_across] + w_far + w_beyond:
@@ -588,10 +677,9 @@
             gather_k.twin_other(dx).wait_send()
 
     for j in travels:
-        for s in range(H):
-            for d in range(2):
-                if s < H - 1 or d == last(j):
-                    ring(d, s, j).wait_send()
+        for s in range(1, H + 1):
+            for d in ways(s, j):
+                ring(d, s, j).wait_send()
     for s in range(H + 1):
         for d in both(s):
             for copy in sides(d, s) + [twin_plane(d, s)]:
@@ -605,10 +693,27 @@
 
     if ends:
 
-        @pl.when((t == 1) | (t == 2))
+        @pl.when(middle)
         def _():
             for i in range(PAIRS):
-                ctx_pass(i, 1).wait_send()
+                ctx_pass(i, 0).wait_send()
+                if i >= turning:
+                    ctx_pass(i, 1).wait_send()
+
+            @pl.when((yh == 0) | jnp.logical_not(rounds))
+            def _():
+                for i in range(turning):
+                    ctx_pass(i, 1).wait_send()
+
+            @pl.when((yh == 0) & rounds)
+            def _():
+                for i in range(turning):
+                    around_on(i).wait_send()
+
+        @pl.when((yh == 1) & rounds & jnp.logical_not(middle))
+        def _():
+            for i in range(turning):
+                around_out(i).wait_send()
 
 
 def rotation_tables(rows, roles):
@@ -656,6 +761,7 @@
             pltpu.VMEM((heads, rows, 128), F32),
             pltpu.VMEM((R, features_out, 128), BF16),
             pltpu.VMEM((NT, heads // 2, rows, 128), BF16),
+            pltpu.VMEM((heads // 2, rows, 128), BF16),
             pltpu.VMEM((features_out, rows), F32),
             dma((2,)),
             dma((3, 9 + 2 * NX)),
@@ -668,6 +774,8 @@
             dma((2, H + 1)),
             dma((heads // 2, NT)),
             dma((heads // 2, NT)),
+            dma((2, heads // 2)),
+            dma((2, heads // 2)),
             dma((heads // 2,)),
         ],
         compiler_params=pltpu.CompilerParams(collective_id=0, has_side_effects=True),

time: 97.8 us -> 89.1 us (0.911)
  Pallas kernels: 95.9 us -> 87.2 us
    pallas_call x1, Pallas kernels: 95.9 us -> 87.2 us  [on_device(): pl.pallas_call(functools.partial(kernel, dims), out_shape=jax.ShapeDtypeS...]
where the time goes in v3:
time: 89.1 us; the launch traced here: 88.9 us
  Pallas kernels  87.2 us (98%)
  local copies, waits for them, and re-layouts  1.75 us (2%)
    pallas_call x1, Pallas kernels, on_device(): pl.pallas_call(functools.partial(kernel, dims), out_shape=jax.ShapeDtypeS...  87.2 us

profile of v3, /device:TPU:57, one launch (start us, length us, event | category | flops | bytes accessed | tf_op | source)
XLA Modules:
  0.0 88.9 jit_solution(13191752852380764615)
XLA Ops:
  0.0 87.2 %layer.1 = bf16[720,256]{1,0:T(8,128)(2,1)} custom-call(bf16[2880,256]{1,0:T(8,128)(2,1)} %bitcast.8, f32[2880]{0:T(1024)} %gain.1, bf16[15,512]{1,0:T(8,128)(2,1)} %wq_in.1, bf16[15,128]{1,0:T(8,128)(2,1)} %wkv_in.1, bf16[720,128]{1,0:T(8,128)(2,1)} %bitcast.9, s32[1,256]{1,0:T(1,128)} %docs_in.1, f32[8]{0:T(128)} %sinks.1, ...), custom_call_target="tpu_custom_call" | custom-call | tf_op jit(solution)/shard_map/layer/pallas_call | solution.py:742
  87.2 1.7 %copy.13 = bf16[1,256,720]{1,2,0:T(8,128)(2,1)} copy(bf16[1,256,720]{1,2,0:T(8,128)(2,1)} %bitcast.7) | data formatting | bytes 737280

commit v4 on v3

--- a/solution.py
+++ b/solution.py
@@ -404,7 +404,11 @@
         gather_k.across().start()
 
     for dx in offsets:
-        gather_k.along(dx).start()
+
+        @pl.when(x + dx < NX)
+        def _(dx=dx):
+            gather_k.along(dx).start()
+
     gather_k.twin_near(0).start()
     o_across.wait_recv()
     for i in range(len(near)):
@@ -454,8 +458,12 @@
     attend(r, STACK, STACK, True)
 
     for dx in offsets:
-        gather_k.along(dx).wait_recv()
-        gather_k.twin_near(dx).start()
+
+        @pl.when(x >= dx)
+        def _(dx=dx):
+            gather_k.along(dx).wait_recv()
+            gather_k.twin_near(dx).start()
+
 
     @pl.when(yh == 1)
     def _():
@@ -465,7 +473,11 @@
         gather_k.twin_other(0).start()
 
     for dx in range(NX):
-        gather_k.twin_near(dx).wait_recv()
+
+        @pl.when(x >= dx)
+        def _(dx=dx):
+            gather_k.twin_near(dx).wait_recv()
+
 
     def near_block(b, _):
         make_bias(b)
@@ -487,8 +499,13 @@
             gather_k.along_other(dx).wait_recv()
             gather_k.twin_other(dx).start()
 
-    o_take_far(0)
-    o_take_sides(1)
+    early = (yh == 0) & (x < NX // 2)
+
+    def o_take():
+        o_take_far(0)
+        o_take_sides(1)
+
+    pl.when(jnp.logical_not(early))(o_take)
 
     far_from = jnp.maximum(r - REACH, 0)
     far_to = jnp.where(yh == 1, HALF, r)
@@ -526,8 +543,9 @@
         return (apart == 1) | ((apart == 2) & jnp.logical_not(middle))
 
     to_end = jnp.where(t == 1, 0, 3)
-    turning = STACK // 2
-    rounds = x < NX // 2
+    def rounds(i):
+        return x < (NX // 2 if i < STACK // 2 else NX // 4)
+
 
     def ctx_pass(i, kind):
         source = 3 - t if kind == 0 else jnp.where(t == 1, 3, 0)
@@ -574,7 +592,7 @@
             ctx[t, i] = jnp.where(low, even, odd).astype(BF16)
             if ends:
 
-                @pl.when((yh == 1) & rounds & jnp.logical_not(middle) & (k == 0))
+                @pl.when((yh == 1) & (x + k * (NX // 4) < NX // 2) & jnp.logical_not(middle))
                 def _(i=i):
                     around_out(i).start()
 
@@ -587,6 +605,7 @@
         return 0
 
     lax.fori_loop(0, 2, finish_stack, 0)
+    pl.when(early)(o_take)
 
     def project(tt):
         total = None
@@ -611,14 +630,12 @@
             for i in range(PAIRS):
                 ctx_copy(i, jnp.where(t == 1, 3, 1)).wait_recv()
                 ctx_pass(i, 0).start()
-                if i >= turning:
-                    relay(i)
-                else:
-                    pl.when((yh == 0) | jnp.logical_not(rounds))(functools.partial(relay, i))
-
-            @pl.when((yh == 0) & rounds)
-            def _():
-                for i in range(turning):
+                pl.when((yh == 0) | jnp.logical_not(rounds(i)))(functools.partial(relay, i))
+
+            for i in range(PAIRS):
+
+                @pl.when((yh == 0) & rounds(i))
+                def _(i=i):
                     around_out(i).wait_recv()
                     around_on(i).start()
 
@@ -638,9 +655,7 @@
         for i in range(PAIRS):
             waited = (t < 0) | (t > NT)
             if ends:
-                passed = dt == 2
-                if i < turning:
-                    passed = passed & ((yh == 0) | jnp.logical_not(rounds))
+                passed = (dt == 2) & ((yh == 0) | jnp.logical_not(rounds(i)))
                 waited = middle & ((source == 1) | (source == 2) | passed)
 
             @pl.when(jnp.logical_not(waited))
@@ -664,10 +679,16 @@
     def _():
         gather_k.across().wait_send()
 
-    for dx in offsets:
-        gather_k.along(dx).wait_send()
     for dx in range(NX):
-        gather_k.twin_near(dx).wait_send()
+
+        @pl.when((x + dx < NX) & (dx > 0))
+        def _(dx=dx):
+            gather_k.along(dx).wait_send()
+
+        @pl.when(x >= dx)
+        def _(dx=dx):
+            gather_k.twin_near(dx).wait_send()
+
 
     @pl.when(yh == 1)
     def _():
@@ -697,22 +718,13 @@
         def _():
             for i in range(PAIRS):
                 ctx_pass(i, 0).wait_send()
-                if i >= turning:
-                    ctx_pass(i, 1).wait_send()
-
-            @pl.when((yh == 0) | jnp.logical_not(rounds))
-            def _():
-                for i in range(turning):
-                    ctx_pass(i, 1).wait_send()
-
-            @pl.when((yh == 0) & rounds)
-            def _():
-                for i in range(turning):
-                    around_on(i).wait_send()
-
-        @pl.when((yh == 1) & rounds & jnp.logical_not(middle))
-        def _():
-            for i in range(turning):
+                pl.when((yh == 0) | jnp.logical_not(rounds(i)))(ctx_pass(i, 1).wait_send)
+                pl.when((yh == 0) & rounds(i))(around_on(i).wait_send)
+
+        for i in range(PAIRS):
+
+            @pl.when((yh == 1) & rounds(i) & jnp.logical_not(middle))
+            def _(i=i):
                 around_out(i).wait_send()
 
 

time: 89.1 us -> 88.8 us (level)
  the two profiles are of different devices: /device:TPU:57 before, /device:TPU:7 now
where the time goes in v4:
time: 88.8 us; the launch traced here: 88.6 us
  Pallas kernels  86.9 us (98%)
  local copies, waits for them, and re-layouts  1.75 us (2%)
    pallas_call x1, Pallas kernels, on_device(): pl.pallas_call(functools.partial(kernel, dims), out_shape=jax.ShapeDtypeS...  86.9 us

profile of v4, /device:TPU:7, one launch (start us, length us, event | category | flops | bytes accessed | tf_op | source)
XLA Modules:
  0.0 88.6 jit_solution(12598200911956854217)
XLA Ops:
  0.0 86.9 %layer.1 = bf16[720,256]{1,0:T(8,128)(2,1)} custom-call(bf16[2880,256]{1,0:T(8,128)(2,1)} %bitcast.8, f32[2880]{0:T(1024)} %gain.1, bf16[15,512]{1,0:T(8,128)(2,1)} %wq_in.1, bf16[15,128]{1,0:T(8,128)(2,1)} %wkv_in.1, bf16[720,128]{1,0:T(8,128)(2,1)} %bitcast.9, s32[1,256]{1,0:T(1,128)} %docs_in.1, f32[8]{0:T(128)} %sinks.1, ...), custom_call_target="tpu_custom_call" | custom-call | tf_op jit(solution)/shard_map/layer/pallas_call | solution.py:754
  86.9 1.7 %copy.13 = bf16[1,256,720]{1,2,0:T(8,128)(2,1)} copy(bf16[1,256,720]{1,2,0:T(8,128)(2,1)} %bitcast.7) | data formatting | bytes 737280
